TPU v7x, 32 devices: a whole 2x2x4 slice. The times are simulated.
32 devices in a mesh: seq: 8 (over z, x), head: 4 (over y, core).
Axes of the slice: x: 2, y: 2, z: 4, core: 2. Of those that a mesh axis runs over, the one named last changes fastest.
Arguments:
- queries: bfloat16 [1024, 3072], P('seq', 'head'), may hold values from -8 to 8
- latents: bfloat16 [1024, 576], P('seq'), may hold values from -8 to 8
- key_up: bfloat16 [512, 2048], P(None, 'head'), may hold values from -0.25 to 0.25
- value_up: bfloat16 [512, 2048], P(None, 'head'), may hold values from -0.25 to 0.25
- out_grad: bfloat16 [1024, 2048], P('seq', 'head'), may hold values from -48 to 48
- positions: int32 [1024], P('seq'), may hold values from 0 to 1023, as said below
Outputs:
- query_grad: bfloat16 [1024, 3072], P('seq', 'head')
- latent_grad: float32 [1024, 576], P('seq')
- key_up_grad: float32 [512, 2048], P(None, 'head')
- value_up_grad: float32 [512, 2048], P(None, 'head')
Inputs may be any that keep to these rules, and one draw needn't show every extreme that they name: Every position from 0 to 1023 occurs once; positions come in stripes of 128 consecutive positions in ascending order, each stripe whole within the rows of one device.
All inputs are finite; a program needn't handle non-finite values.
Results may differ from a plain program's by a relative error of at most 0.0084.
Values may be sent and summed in bfloat16 or wider, within the bound.
A program may use at most 64 MiB of HBM per device.

v0:
```python
import math
import jax
import jax.numpy as jnp
from jax import lax
from jax.sharding import PartitionSpec as P

D_LAT = 512
D_ROPE = 64
D_NOPE = 128
D_V = 128
NEG = -1e30


def shifted(value, axis, steps):
    count = lax.axis_size(axis)
    pairs = [(source, (source + steps) % count) for source in range(count)]
    return lax.ppermute(value, axis, pairs)


def up_project(block, key_up, value_up):
    compressed = block[:, :D_LAT]
    key_nope = jnp.dot(compressed, key_up, preferred_element_type=jnp.float32).astype(jnp.bfloat16)
    values = jnp.dot(compressed, value_up, preferred_element_type=jnp.float32).astype(jnp.bfloat16)
    return (key_nope, block[:, D_LAT:], values)


def split_heads(queries, out_grad, key_nope, values):
    heads = key_nope.shape[1] // D_NOPE
    shaped = queries.reshape(queries.shape[0], heads, D_NOPE + D_ROPE)
    grads = out_grad.reshape(out_grad.shape[0], heads, D_V)
    key3 = key_nope.reshape(key_nope.shape[0], heads, D_NOPE)
    value3 = values.reshape(values.shape[0], heads, D_V)
    return (shaped[:, :, :D_NOPE], shaped[:, :, D_NOPE:], grads, key3, value3)


def scores_of(q_nope, q_rope, key3, rope_keys, query_pos, key_pos):
    scale = 1.0 / math.sqrt(D_NOPE + D_ROPE)
    raw = jnp.einsum("bhd,khd->hbk", q_nope, key3, preferred_element_type=jnp.float32)
    raw = raw + jnp.einsum("bhd,kd->hbk", q_rope, rope_keys, preferred_element_type=jnp.float32)
    visible = (key_pos[None, :] <= query_pos[:, None])[None]
    return (raw * scale, visible)


def forward_update(stats, queries, out_grad, query_pos, key_nope, rope_keys, values, key_pos):
    top, total, weighted = stats
    q_nope, q_rope, grads, key3, value3 = split_heads(queries, out_grad, key_nope, values)
    scores, visible = scores_of(q_nope, q_rope, key3, rope_keys, query_pos, key_pos)
    dprobs = jnp.einsum("bhd,khd->hbk", grads, value3, preferred_element_type=jnp.float32)
    masked = jnp.where(visible, scores, NEG)
    new_top = jnp.maximum(top, jnp.max(masked, axis=2))
    weights = jnp.exp(jnp.where(visible, scores - new_top[:, :, None], NEG))
    fade = jnp.exp(top - new_top)
    total = total * fade + jnp.sum(weights, axis=2)
    weighted = weighted * fade + jnp.sum(weights * dprobs, axis=2)
    return (new_top, total, weighted)


def backward_terms(queries, out_grad, query_pos, lse, delta, key_nope, rope_keys, values, key_pos):
    scale = 1.0 / math.sqrt(D_NOPE + D_ROPE)
    q_nope, q_rope, grads, key3, value3 = split_heads(queries, out_grad, key_nope, values)
    scores, visible = scores_of(q_nope, q_rope, key3, rope_keys, query_pos, key_pos)
    probs = jnp.exp(jnp.where(visible, scores - lse[:, :, None], NEG))
    dprobs = jnp.einsum("bhd,khd->hbk", grads, value3, preferred_element_type=jnp.float32)
    dscore = (probs * (dprobs - delta[:, :, None]) * scale).astype(jnp.bfloat16)
    probs16 = probs.astype(jnp.bfloat16)
    grad_nope = jnp.einsum("hbk,khd->bhd", dscore, key3, preferred_element_type=jnp.float32)
    grad_rope = jnp.einsum("hbk,kd->bhd", dscore, rope_keys, preferred_element_type=jnp.float32)
    q_grad = jnp.concatenate([grad_nope, grad_rope], axis=2).reshape(queries.shape[0], -1)
    key_part = jnp.einsum("hbk,bhd->khd", dscore, q_nope, preferred_element_type=jnp.float32)
    value_part = jnp.einsum("hbk,bhd->khd", probs16, grads, preferred_element_type=jnp.float32)
    rope_part = jnp.einsum("hbk,bhd->kd", dscore, q_rope, preferred_element_type=jnp.float32)
    key_rows = key3.shape[0]
    part = jnp.concatenate(
        [key_part.reshape(key_rows, -1), value_part.reshape(key_rows, -1), rope_part], axis=1
    )
    return (q_grad, part)


def shards(queries, latents, key_up, value_up, out_grad, positions):
    rows = queries.shape[0]
    heads = key_up.shape[1] // D_NOPE
    qcols = queries.shape[1]
    nseq = lax.axis_size("seq")
    here = lax.axis_index("seq")
    every_pos = lax.all_gather(positions, "seq", axis=0, tiled=True)
    part_width = heads * (D_NOPE + D_V) + D_ROPE

    def owner_start(step):
        return (here - step) % nseq * rows

    def owner_pos(step):
        return lax.dynamic_slice_in_dim(every_pos, owner_start(step), rows, 0)

    start_stats = (
        jnp.full((heads, rows), NEG, jnp.float32),
        jnp.zeros((heads, rows), jnp.float32),
        jnp.zeros((heads, rows), jnp.float32),
    )
    zero_grads = jnp.zeros((rows, part_width), jnp.float32)
    zero_query = jnp.zeros((rows, qcols), jnp.float32)

    def fold_block(stats, block, start):
        key_nope, rope_keys, values = up_project(block, key_up, value_up)
        key_pos = lax.dynamic_slice_in_dim(every_pos, start, block.shape[0], 0)
        return forward_update(
            stats, queries, out_grad, positions, key_nope, rope_keys, values, key_pos
        )

    def grad_block(block, grads, q_acc, step, lse, delta):
        key_nope, rope_keys, values = up_project(block, key_up, value_up)
        q_grad, part = backward_terms(
            queries, out_grad, positions, lse, delta, key_nope, rope_keys, values, owner_pos(step)
        )
        return (grads + part, q_acc + q_grad)

    gathered = lax.all_gather(latents, "seq", axis=0, tiled=True)
    count = gathered.shape[0]
    width = math.gcd(count, 512)

    def turn(index, carry):
        block = lax.dynamic_slice_in_dim(gathered, index * width, width, 0)
        return fold_block(carry, block, index * width)

    top, total, weighted = lax.fori_loop(0, count // width, turn, start_stats)
    lse = top + jnp.log(total)
    delta = weighted / total

    def kept_turn(step, carry):
        grads, q_acc = carry
        block = lax.dynamic_slice_in_dim(gathered, owner_start(step), rows, 0)
        grads, q_acc = grad_block(block, grads, q_acc, step, lse, delta)
        grads = shifted(grads, "seq", 1)
        return (grads, q_acc)

    grads, q_acc = lax.fori_loop(0, nseq - 1, kept_turn, (zero_grads, zero_query))
    last_block = lax.dynamic_slice_in_dim(gathered, owner_start(nseq - 1), rows, 0)
    grads, q_acc = grad_block(last_block, grads, q_acc, nseq - 1, lse, delta)
    key_grads = shifted(grads, "seq", 1)
    split_one = heads * D_NOPE
    split_two = split_one + heads * D_V
    key_grad = key_grads[:, :split_one]
    value_grad = key_grads[:, split_one:split_two]
    high = lax.Precision.HIGHEST
    key_up32 = key_up.astype(jnp.float32)
    value_up32 = value_up.astype(jnp.float32)
    inner = (((1,), (1,)), ((), ()))
    folded = lax.dot_general(key_grad, key_up32, inner, precision=high)
    folded = folded + lax.dot_general(value_grad, value_up32, inner, precision=high)
    latent_part = jnp.concatenate([folded, key_grads[:, split_two:]], axis=1)
    latent_grad = lax.psum(latent_part, "head")
    compressed = latents[:, :D_LAT].astype(jnp.float32)
    outer = (((0,), (0,)), ((), ()))
    key_term = lax.dot_general(compressed, key_grad, outer, precision=high)
    value_term = lax.dot_general(compressed, value_grad, outer, precision=high)
    key_up_grad, value_up_grad = lax.psum((key_term, value_term), "seq")
    return (q_acc.astype(jnp.bfloat16), latent_grad, key_up_grad, value_up_grad)


def solution(mesh):
    in_specs = (
        P("seq", "head"),
        P("seq", None),
        P(None, "head"),
        P(None, "head"),
        P("seq", "head"),
        P("seq"),
    )
    out_specs = (P("seq", "head"), P("seq", None), P(None, "head"), P(None, "head"))
    return jax.shard_map(shards, mesh=mesh, in_specs=in_specs, out_specs=out_specs, check_vma=False)
```

profile of v0, /device:TPU:0, one launch (start us, length us, event | category | flops | bytes accessed | tf_op | source)
XLA Modules:
  0.0 364.3 jit_solution(10623151957692037776)
XLA Ops:
  10.2 22.5 %all-gather = s32[8,1,128]{2,1,0:T(1,128)S(1)} all-gather(s32[1,1,128]{2,1,0:T(1,128)} %bitcast.257), channel_id=1, replica_groups=mesh['seq'=8,'head'=4] {'seq'}, dimensions={0}, use_global_device_ids=true | all-gather | bytes 4608 | tf_op jit(solution)/shard_map/all_gather | solution.py:85
  33.5 19.7 %all-gather.3.cloned.1.call-done = bf16[1024,576]{0,1:T(8,128)(2,1)} async-done(((bf16[128,576]{0,1:T(8,128)(2,1)}), bf16[1024,576]{0,1:T(8,128)(2,1)}) %all-gather.3.cloned.1.call-update) | async-done | bytes 1179664 | tf_op jit(solution)/shard_map/all_gather | solution.py:116
  53.2 1.4 convolution_convert_fusion.5
  54.8 7.6 %while.36 = (s32[]{:T(128)}, f32[4,128]{1,0:T(4,128)S(1)}, f32[4,128]{1,0:T(4,128)S(1)}, f32[4,128]{1,0:T(4,128)S(1)}, s32[1024]{0:T(1024)S(1)}, /*index=5*/s32[...) while((s32[]{:T(128)}, f32[4,128]{1,0:T(4,128)S(1)}, ...), condition=%wide.region_4.5_spmd.clone, body=%wide.region_0.4_spmd.clone.sunk | while | flops 708120064 | bytes 14854930 | solution.py:124
  55.0 1.6 convolution_convert_fusion.10
  58.8 1.6 convolution_convert_fusion.10
  63.8 1.2 fusion.47
  66.3 135.5 %while.37 = (s32[]{:T(128)}, f32[128,1088]{0,1:T(8,128)S(1)}, f32[128,768]{0,1:T(8,128)S(1)}, s32[]{:T(128)}, s32[1024]{0:T(1024)S(1)}, /*index=5*/s32[128]{0:T(...) while((s32[]{:T(128)}, f32[128,1088]{0,1:T(8,128)S(1)}, ...), condition=%wide.region_6.7_spmd.clone, body=%wide.region_5.6_spmd.clone.sunk | while | flops 244719632 | bytes 11737526 | solution.py:135
  71.8 1.4 collective-permute-start
  74.4 12.3 %collective-permute-done = f32[128,1088]{0,1:T(8,128)S(1)} collective-permute-done((f32[128,1088]{0,1:T(8,128)}, f32[128,1088]{0,1:T(8,128)S(1)}, u32[]{:S(2)}, u32[]{:S(2)}) %collective-permute-start) | collective-permute-done | bytes 557088 | tf_op jit(solution)/shard_map/while/body/eval_jaxpr/ppermute | solution.py:17
  94.5 12.9 %collective-permute-done = f32[128,1088]{0,1:T(8,128)S(1)} collective-permute-done((f32[128,1088]{0,1:T(8,128)}, f32[128,1088]{0,1:T(8,128)S(1)}, u32[]{:S(2)}, u32[]{:S(2)}) %collective-permute-start) | collective-permute-done | bytes 557088 | tf_op jit(solution)/shard_map/while/body/eval_jaxpr/ppermute | solution.py:17
  114.0 13.2 %collective-permute-done = f32[128,1088]{0,1:T(8,128)S(1)} collective-permute-done((f32[128,1088]{0,1:T(8,128)}, f32[128,1088]{0,1:T(8,128)S(1)}, u32[]{:S(2)}, u32[]{:S(2)}) %collective-permute-start) | collective-permute-done | bytes 557088 | tf_op jit(solution)/shard_map/while/body/eval_jaxpr/ppermute | solution.py:17
  133.9 12.4 %collective-permute-done = f32[128,1088]{0,1:T(8,128)S(1)} collective-permute-done((f32[128,1088]{0,1:T(8,128)}, f32[128,1088]{0,1:T(8,128)S(1)}, u32[]{:S(2)}, u32[]{:S(2)}) %collective-permute-start) | collective-permute-done | bytes 557088 | tf_op jit(solution)/shard_map/while/body/eval_jaxpr/ppermute | solution.py:17
  152.9 11.5 %collective-permute-done = f32[128,1088]{0,1:T(8,128)S(1)} collective-permute-done((f32[128,1088]{0,1:T(8,128)}, f32[128,1088]{0,1:T(8,128)S(1)}, u32[]{:S(2)}, u32[]{:S(2)}) %collective-permute-start) | collective-permute-done | bytes 557088 | tf_op jit(solution)/shard_map/while/body/eval_jaxpr/ppermute | solution.py:17
  171.1 11.3 %collective-permute-done = f32[128,1088]{0,1:T(8,128)S(1)} collective-permute-done((f32[128,1088]{0,1:T(8,128)}, f32[128,1088]{0,1:T(8,128)S(1)}, u32[]{:S(2)}, u32[]{:S(2)}) %collective-permute-start) | collective-permute-done | bytes 557088 | tf_op jit(solution)/shard_map/while/body/eval_jaxpr/ppermute | solution.py:17
  189.0 12.8 %collective-permute-done = f32[128,1088]{0,1:T(8,128)S(1)} collective-permute-done((f32[128,1088]{0,1:T(8,128)}, f32[128,1088]{0,1:T(8,128)S(1)}, u32[]{:S(2)}, u32[]{:S(2)}) %collective-permute-start) | collective-permute-done | bytes 557088 | tf_op jit(solution)/shard_map/while/body/eval_jaxpr/ppermute | solution.py:17
  202.9 12.2 %collective-permute-done.1 = f32[128,1088]{0,1:T(8,128)S(1)} collective-permute-done((f32[128,1088]{0,1:T(8,128)S(1)}, f32[128,1088]{0,1:T(8,128)S(1)}, u32[]{:S(2)}, u32[]{:S(2)}) %collective-permute-start.1) | collective-permute-done | bytes 557088 | tf_op jit(solution)/shard_map/ppermute | solution.py:17
  217.4 1.6 convolution_bitcast_fusion.9
  219.0 1.5 convolution_bitcast_fusion.8
  222.7 24.6 %all-reduce.4.cloned.1.call-done = f32[128,576]{1,0:T(8,128)} async-done(((f32[128,576]{1,0:T(8,128)}), f32[128,576]{1,0:T(8,128)}) %all-reduce.4.cloned.1.call-update) | async-done | bytes 294928 | tf_op jit(solution)/shard_map/psum | solution.py:150
  247.3 1.8 copy.123
  249.1 104.7 %all-reduce.6.cloned.1.call-done = (f32[512,512]{0,1:T(8,128)}, f32[512,512]{0,1:T(8,128)}) async-done(((f32[512,512]{0,1:T(8,128)}, f32[512,512]{0,1:T(8,128)}), (f32[512,512]{0,1:T(8,128)}, f32[512,512]{0,1:T(8,128)})) %all-reduce.6.cloned.1.call-update) | async-done | bytes 2097168 | tf_op jit(solution)/shard_map/psum | solution.py:155
  353.9 2.6 copy.124
  356.5 1.3 copy.125
  (190 shorter events, 63.3 us)
Async XLA Ops:
  7.2 47.6 %copy-start.5 = (bf16[128,512]{1,0:T(8,128)(2,1)S(1)}, bf16[128,512]{1,0:T(8,128)(2,1)}, u32[]{:S(2)}) copy-start(bf16[128,512]{1,0:T(8,128)(2,1)} %param.14) | copy-start | bytes 393220
  7.2 47.6 %copy-start.6 = (s32[128]{0:T(128)S(1)}, s32[128]{0:T(128)}, u32[]{:S(2)}) copy-start(s32[128]{0:T(128)} %param.15) | copy-start | bytes 1540
  7.2 47.6 %copy-start.1 = (bf16[512,512]{1,0:T(8,128)(2,1)S(1)}, bf16[512,512]{1,0:T(8,128)(2,1)}, u32[]{:S(2)}) copy-start(bf16[512,512]{1,0:T(8,128)(2,1)} %param.12) | copy-start | bytes 1572868
  7.2 47.6 %copy-start = (bf16[512,512]{1,0:T(8,128)(2,1)S(1)}, bf16[512,512]{1,0:T(8,128)(2,1)}, u32[]{:S(2)}) copy-start(bf16[512,512]{1,0:T(8,128)(2,1)} %param.13) | copy-start | bytes 1572868
  7.2 46.0 %all-gather.3.cloned.1.call-start = ((), (), s32[]{:S(2)}) async-start(), calls=%async_computation | async-start | bytes 1327104 | tf_op jit(solution)/shard_map/all_gather | solution.py:116
  7.9 239.3 %all-reduce.4.cloned.1.call-start = ((), (), s32[]{:S(2)}) async-start(), calls=%async_computation.1 | async-start | bytes 655360 | tf_op jit(solution)/shard_map/psum | solution.py:150
  54.8 1.9 copy-start.2
  58.6 1.9 copy-start.2
  71.8 14.8 %collective-permute-start = (f32[128,1088]{0,1:T(8,128)}, f32[128,1088]{0,1:T(8,128)S(1)}, u32[]{:S(2)}, u32[]{:S(2)}) collective-permute-start(f32[128,1088]{0,1:T(8,128)} %maximum_add_fusion.3), channel_id=1, source_target_pairs={{0,4},{4,8},{8,12},{12,16},{16,20},{20,24},{24,28},{28,0},{1,5},{5... | collective-permute-start | bytes 1671176 | tf_op jit(solution)/shard_map/while/body/eval_jaxpr/ppermute | solution.py:17
  92.1 15.2 %collective-permute-start = (f32[128,1088]{0,1:T(8,128)}, f32[128,1088]{0,1:T(8,128)S(1)}, u32[]{:S(2)}, u32[]{:S(2)}) collective-permute-start(f32[128,1088]{0,1:T(8,128)} %maximum_add_fusion.3), channel_id=1, source_target_pairs={{0,4},{4,8},{8,12},{12,16},{16,20},{20,24},{24,28},{28,0},{1,5},{5... | collective-permute-start | bytes 1671176 | tf_op jit(solution)/shard_map/while/body/eval_jaxpr/ppermute | solution.py:17
  112.9 14.4 %collective-permute-start = (f32[128,1088]{0,1:T(8,128)}, f32[128,1088]{0,1:T(8,128)S(1)}, u32[]{:S(2)}, u32[]{:S(2)}) collective-permute-start(f32[128,1088]{0,1:T(8,128)} %maximum_add_fusion.3), channel_id=1, source_target_pairs={{0,4},{4,8},{8,12},{12,16},{16,20},{20,24},{24,28},{28,0},{1,5},{5... | collective-permute-start | bytes 1671176 | tf_op jit(solution)/shard_map/while/body/eval_jaxpr/ppermute | solution.py:17
  132.7 13.5 %collective-permute-start = (f32[128,1088]{0,1:T(8,128)}, f32[128,1088]{0,1:T(8,128)S(1)}, u32[]{:S(2)}, u32[]{:S(2)}) collective-permute-start(f32[128,1088]{0,1:T(8,128)} %maximum_add_fusion.3), channel_id=1, source_target_pairs={{0,4},{4,8},{8,12},{12,16},{16,20},{20,24},{24,28},{28,0},{1,5},{5... | collective-permute-start | bytes 1671176 | tf_op jit(solution)/shard_map/while/body/eval_jaxpr/ppermute | solution.py:17
  151.7 12.7 %collective-permute-start = (f32[128,1088]{0,1:T(8,128)}, f32[128,1088]{0,1:T(8,128)S(1)}, u32[]{:S(2)}, u32[]{:S(2)}) collective-permute-start(f32[128,1088]{0,1:T(8,128)} %maximum_add_fusion.3), channel_id=1, source_target_pairs={{0,4},{4,8},{8,12},{12,16},{16,20},{20,24},{24,28},{28,0},{1,5},{5... | collective-permute-start | bytes 1671176 | tf_op jit(solution)/shard_map/while/body/eval_jaxpr/ppermute | solution.py:17
  169.9 12.4 %collective-permute-start = (f32[128,1088]{0,1:T(8,128)}, f32[128,1088]{0,1:T(8,128)S(1)}, u32[]{:S(2)}, u32[]{:S(2)}) collective-permute-start(f32[128,1088]{0,1:T(8,128)} %maximum_add_fusion.3), channel_id=1, source_target_pairs={{0,4},{4,8},{8,12},{12,16},{16,20},{20,24},{24,28},{28,0},{1,5},{5... | collective-permute-start | bytes 1671176 | tf_op jit(solution)/shard_map/while/body/eval_jaxpr/ppermute | solution.py:17
  187.8 14.0 %collective-permute-start = (f32[128,1088]{0,1:T(8,128)}, f32[128,1088]{0,1:T(8,128)S(1)}, u32[]{:S(2)}, u32[]{:S(2)}) collective-permute-start(f32[128,1088]{0,1:T(8,128)} %maximum_add_fusion.3), channel_id=1, source_target_pairs={{0,4},{4,8},{8,12},{12,16},{16,20},{20,24},{24,28},{28,0},{1,5},{5... | collective-permute-start | bytes 1671176 | tf_op jit(solution)/shard_map/while/body/eval_jaxpr/ppermute | solution.py:17
  202.8 12.3 %collective-permute-start.1 = (f32[128,1088]{0,1:T(8,128)S(1)}, f32[128,1088]{0,1:T(8,128)S(1)}, u32[]{:S(2)}, u32[]{:S(2)}) collective-permute-start(f32[128,1088]{0,1:T(8,128)S(1)} %maximum_add_fusion.1), channel_id=1, source_target_pairs={{0,4},{4,8},{8,12},{12,16},{16,20},{20,24},{24,28},{28,0},{1,5},{5... | collective-permute-start | bytes 1671176 | tf_op jit(solution)/shard_map/ppermute | solution.py:17
  215.9 1.6 copy-start.3
  217.4 136.5 %all-reduce.6.cloned.1.call-start = ((), (), s32[]{:S(2)}) async-start(), calls=%async_computation.2 | async-start | bytes 4194304 | tf_op jit(solution)/shard_map/psum | solution.py:155
  353.9 2.6 copy-start.4
Sparse Core Ops, SparseCore 0:
  10.1 43.1 all-gather.2
  217.5 29.7 all-reduce.3
  251.5 102.2 all-reduce.5
where the time goes:
time: 366 us; the launch traced here: 364 us
  waiting for transfers between devices  248 us (68%)
  matrix products  54.3 us (15%)
  blocking collectives  22.5 us (6%)
  between operations  14.1 us (4%)
  other arithmetic  11.5 us (3%)
  local copies, waits for them, and re-layouts  10.1 us (3%)
    psum x1, waiting for transfers between devices, shards(): key_up_grad, value_up_grad = lax.psum((key_term, value_term), 'seq')  105 us
    ppermute x8, waiting for transfers between devices, shifted(): return lax.ppermute(value, axis, pairs)  98.6 us
    psum x1, waiting for transfers between devices, shards(): latent_grad = lax.psum(latent_part, 'head')  24.6 us
    all_gather x1, blocking collectives, shards(): every_pos = lax.all_gather(positions, 'seq', axis=0, tiled=True)  22.5 us
    all_gather x1, waiting for transfers between devices, shards(): gathered = lax.all_gather(latents, 'seq', axis=0, tiled=True)  19.7 us
    dot_general x10, matrix products, up_project(): jnp.dot(compressed, value_up, preferred_element_type=jnp.float32)  12.5 us
    dot_general x10, matrix products, up_project(): jnp.dot(compressed, key_up, preferred_element_type=jnp.float32)  10.5 us
    dot_general x10, matrix products, scores_of(): jnp.einsum('bhd,kd->hbk', q_rope, rope_keys, preferred_element_type=jnp.f...  8.11 us
  transfers between devices with their start and end apart: 11, of which 11 were waited for; matrix products, arithmetic and copies ran while one was open for 5% of the time, Pallas kernels for 0%

commit v1 on v0

--- a/solution.py
+++ b/solution.py
@@ -147,7 +147,8 @@
     folded = lax.dot_general(key_grad, key_up32, inner, precision=high)
     folded = folded + lax.dot_general(value_grad, value_up32, inner, precision=high)
     latent_part = jnp.concatenate([folded, key_grads[:, split_two:]], axis=1)
-    latent_grad = lax.psum(latent_part, "head")
+    parts = lax.all_gather(latent_part, "head", axis=0, tiled=False)
+    latent_grad = parts.sum(axis=0)
     compressed = latents[:, :D_LAT].astype(jnp.float32)
     outer = (((0,), (0,)), ((), ()))
     key_term = lax.dot_general(compressed, key_grad, outer, precision=high)

time: 366 us -> 351 us (0.959)
  waiting for transfers between devices: 248 us -> 233 us
    psum x1 -> x0, waiting for transfers between devices: 24.6 us -> none  [shards(): latent_grad = lax.psum(latent_part, 'head')]
    all_gather x0 -> x1, waiting for transfers between devices: none -> 10.2 us  [shards(): parts = lax.all_gather(latent_part, 'head', axis=0, tiled=False)]
where the time goes in v1:
time: 351 us; the launch traced here: 350 us
  waiting for transfers between devices  233 us (66%)
  matrix products  54.4 us (15%)
  blocking collectives  22.5 us (6%)
  between operations  14.1 us (4%)
  other arithmetic  12.9 us (4%)
  local copies, waits for them, and re-layouts  9.09 us (3%)
    psum x1, waiting for transfers between devices, shards(): key_up_grad, value_up_grad = lax.psum((key_term, value_term), 'seq')  104 us
    ppermute x8, waiting for transfers between devices, shifted(): return lax.ppermute(value, axis, pairs)  98.6 us
    all_gather x1, blocking collectives, shards(): every_pos = lax.all_gather(positions, 'seq', axis=0, tiled=True)  22.5 us
    all_gather x1, waiting for transfers between devices, shards(): gathered = lax.all_gather(latents, 'seq', axis=0, tiled=True)  19.7 us
    dot_general x10, matrix products, up_project(): jnp.dot(compressed, value_up, preferred_element_type=jnp.float32)  12.5 us
    dot_general x10, matrix products, up_project(): jnp.dot(compressed, key_up, preferred_element_type=jnp.float32)  10.5 us
    all_gather x1, waiting for transfers between devices, shards(): parts = lax.all_gather(latent_part, 'head', axis=0, tiled=False)  10.2 us
    dot_general x10, matrix products, scores_of(): jnp.einsum('bhd,kd->hbk', q_rope, rope_keys, preferred_element_type=jnp.f...  8.12 us
  transfers between devices with their start and end apart: 11, of which 11 were waited for; matrix products, arithmetic and copies ran while one was open for 5% of the time, Pallas kernels for 0%

profile of v1, /device:TPU:0, one launch (start us, length us, event | category | flops | bytes accessed | tf_op | source)
XLA Modules:
  0.0 349.9 jit_solution(1629887168160353393)
XLA Ops:
  10.2 22.5 %all-gather.1 = s32[8,1,128]{2,1,0:T(1,128)S(1)} all-gather(s32[1,1,128]{2,1,0:T(1,128)} %bitcast.259), channel_id=1, replica_groups=mesh['seq'=8,'head'=4] {'seq'}, dimensions={0}, use_global_device_ids=true | all-gather | bytes 4608 | tf_op jit(solution)/shard_map/all_gather | solution.py:85
  33.5 19.7 %all-gather.5.cloned.1.call-done = bf16[1024,576]{0,1:T(8,128)(2,1)} async-done(((bf16[128,576]{0,1:T(8,128)(2,1)}), bf16[1024,576]{0,1:T(8,128)(2,1)}) %all-gather.5.cloned.1.call-update) | async-done | bytes 1179664 | tf_op jit(solution)/shard_map/all_gather | solution.py:116
  53.2 1.4 convolution_convert_fusion.5
  54.8 7.6 %while.36 = (s32[]{:T(128)}, f32[4,128]{1,0:T(4,128)S(1)}, f32[4,128]{1,0:T(4,128)S(1)}, f32[4,128]{1,0:T(4,128)S(1)}, s32[1024]{0:T(1024)S(1)}, /*index=5*/s32[...) while((s32[]{:T(128)}, f32[4,128]{1,0:T(4,128)S(1)}, ...), condition=%wide.region_4.5_spmd.clone, body=%wide.region_0.4_spmd.clone.sunk | while | flops 708120064 | bytes 14854930 | solution.py:124
  55.0 1.6 convolution_convert_fusion.10
  58.8 1.6 convolution_convert_fusion.10
  63.8 1.2 fusion.47
  66.3 135.5 %while.37 = (s32[]{:T(128)}, f32[128,1088]{0,1:T(8,128)S(1)}, f32[128,768]{0,1:T(8,128)S(1)}, s32[]{:T(128)}, s32[1024]{0:T(1024)S(1)}, /*index=5*/s32[128]{0:T(...) while((s32[]{:T(128)}, f32[128,1088]{0,1:T(8,128)S(1)}, ...), condition=%wide.region_6.7_spmd.clone, body=%wide.region_5.6_spmd.clone.sunk | while | flops 244719632 | bytes 11737526 | solution.py:135
  71.8 1.4 collective-permute-start
  74.4 12.3 %collective-permute-done = f32[128,1088]{0,1:T(8,128)S(1)} collective-permute-done((f32[128,1088]{0,1:T(8,128)}, f32[128,1088]{0,1:T(8,128)S(1)}, u32[]{:S(2)}, u32[]{:S(2)}) %collective-permute-start) | collective-permute-done | bytes 557088 | tf_op jit(solution)/shard_map/while/body/eval_jaxpr/ppermute | solution.py:17
  94.5 12.9 %collective-permute-done = f32[128,1088]{0,1:T(8,128)S(1)} collective-permute-done((f32[128,1088]{0,1:T(8,128)}, f32[128,1088]{0,1:T(8,128)S(1)}, u32[]{:S(2)}, u32[]{:S(2)}) %collective-permute-start) | collective-permute-done | bytes 557088 | tf_op jit(solution)/shard_map/while/body/eval_jaxpr/ppermute | solution.py:17
  114.0 13.2 %collective-permute-done = f32[128,1088]{0,1:T(8,128)S(1)} collective-permute-done((f32[128,1088]{0,1:T(8,128)}, f32[128,1088]{0,1:T(8,128)S(1)}, u32[]{:S(2)}, u32[]{:S(2)}) %collective-permute-start) | collective-permute-done | bytes 557088 | tf_op jit(solution)/shard_map/while/body/eval_jaxpr/ppermute | solution.py:17
  133.9 12.3 %collective-permute-done = f32[128,1088]{0,1:T(8,128)S(1)} collective-permute-done((f32[128,1088]{0,1:T(8,128)}, f32[128,1088]{0,1:T(8,128)S(1)}, u32[]{:S(2)}, u32[]{:S(2)}) %collective-permute-start) | collective-permute-done | bytes 557088 | tf_op jit(solution)/shard_map/while/body/eval_jaxpr/ppermute | solution.py:17
  152.9 11.5 %collective-permute-done = f32[128,1088]{0,1:T(8,128)S(1)} collective-permute-done((f32[128,1088]{0,1:T(8,128)}, f32[128,1088]{0,1:T(8,128)S(1)}, u32[]{:S(2)}, u32[]{:S(2)}) %collective-permute-start) | collective-permute-done | bytes 557088 | tf_op jit(solution)/shard_map/while/body/eval_jaxpr/ppermute | solution.py:17
  171.0 11.3 %collective-permute-done = f32[128,1088]{0,1:T(8,128)S(1)} collective-permute-done((f32[128,1088]{0,1:T(8,128)}, f32[128,1088]{0,1:T(8,128)S(1)}, u32[]{:S(2)}, u32[]{:S(2)}) %collective-permute-start) | collective-permute-done | bytes 557088 | tf_op jit(solution)/shard_map/while/body/eval_jaxpr/ppermute | solution.py:17
  189.0 12.8 %collective-permute-done = f32[128,1088]{0,1:T(8,128)S(1)} collective-permute-done((f32[128,1088]{0,1:T(8,128)}, f32[128,1088]{0,1:T(8,128)S(1)}, u32[]{:S(2)}, u32[]{:S(2)}) %collective-permute-start) | collective-permute-done | bytes 557088 | tf_op jit(solution)/shard_map/while/body/eval_jaxpr/ppermute | solution.py:17
  202.8 12.2 %collective-permute-done.1 = f32[128,1088]{0,1:T(8,128)S(1)} collective-permute-done((f32[128,1088]{0,1:T(8,128)S(1)}, f32[128,1088]{0,1:T(8,128)S(1)}, u32[]{:S(2)}, u32[]{:S(2)}) %collective-permute-start.1) | collective-permute-done | bytes 557088 | tf_op jit(solution)/shard_map/ppermute | solution.py:17
  217.4 1.6 convolution_bitcast_fusion.9
  219.0 1.6 convolution_bitcast_fusion.8
  222.7 10.2 %all-gather.7.cloned.1.call-done = f32[512,576]{1,0:T(8,128)} async-done(((f32[128,576]{1,0:T(8,128)}), f32[512,576]{1,0:T(8,128)}) %all-gather.7.cloned.1.call-update) | async-done | bytes 1179664 | tf_op jit(solution)/shard_map/all_gather | solution.py:150
  232.9 1.4 reduce_sum.35
  235.2 104.3 %all-reduce.3.cloned.1.call-done = (f32[512,512]{0,1:T(8,128)}, f32[512,512]{0,1:T(8,128)}) async-done(((f32[512,512]{0,1:T(8,128)}, f32[512,512]{0,1:T(8,128)}), (f32[512,512]{0,1:T(8,128)}, f32[512,512]{0,1:T(8,128)})) %all-reduce.3.cloned.1.call-update) | async-done | bytes 2097168 | tf_op jit(solution)/shard_map/psum | solution.py:156
  339.5 2.6 copy.122
  342.1 1.3 copy.123
  (191 shorter events, 64.1 us)
Async XLA Ops:
  7.2 47.6 %copy-start.5 = (bf16[128,512]{1,0:T(8,128)(2,1)S(1)}, bf16[128,512]{1,0:T(8,128)(2,1)}, u32[]{:S(2)}) copy-start(bf16[128,512]{1,0:T(8,128)(2,1)} %param.14) | copy-start | bytes 393220
  7.2 47.6 %copy-start.6 = (s32[128]{0:T(128)S(1)}, s32[128]{0:T(128)}, u32[]{:S(2)}) copy-start(s32[128]{0:T(128)} %param.15) | copy-start | bytes 1540
  7.2 47.6 %copy-start.1 = (bf16[512,512]{1,0:T(8,128)(2,1)S(1)}, bf16[512,512]{1,0:T(8,128)(2,1)}, u32[]{:S(2)}) copy-start(bf16[512,512]{1,0:T(8,128)(2,1)} %param.12) | copy-start | bytes 1572868
  7.2 47.6 %copy-start = (bf16[512,512]{1,0:T(8,128)(2,1)S(1)}, bf16[512,512]{1,0:T(8,128)(2,1)}, u32[]{:S(2)}) copy-start(bf16[512,512]{1,0:T(8,128)(2,1)} %param.13) | copy-start | bytes 1572868
  7.2 46.0 %all-gather.5.cloned.1.call-start = ((), (), s32[]{:S(2)}) async-start(), calls=%async_computation | async-start | bytes 1327104 | tf_op jit(solution)/shard_map/all_gather | solution.py:116
  7.9 225.0 %all-gather.7.cloned.1.call-start = ((), (), s32[]{:S(2)}) async-start(), calls=%async_computation.1 | async-start | bytes 1638400 | tf_op jit(solution)/shard_map/all_gather | solution.py:150
  54.8 1.9 copy-start.2
  58.6 1.9 copy-start.2
  71.8 14.8 %collective-permute-start = (f32[128,1088]{0,1:T(8,128)}, f32[128,1088]{0,1:T(8,128)S(1)}, u32[]{:S(2)}, u32[]{:S(2)}) collective-permute-start(f32[128,1088]{0,1:T(8,128)} %maximum_add_fusion.3), channel_id=1, source_target_pairs={{0,4},{4,8},{8,12},{12,16},{16,20},{20,24},{24,28},{28,0},{1,5},{5... | collective-permute-start | bytes 1671176 | tf_op jit(solution)/shard_map/while/body/eval_jaxpr/ppermute | solution.py:17
  92.1 15.2 %collective-permute-start = (f32[128,1088]{0,1:T(8,128)}, f32[128,1088]{0,1:T(8,128)S(1)}, u32[]{:S(2)}, u32[]{:S(2)}) collective-permute-start(f32[128,1088]{0,1:T(8,128)} %maximum_add_fusion.3), channel_id=1, source_target_pairs={{0,4},{4,8},{8,12},{12,16},{16,20},{20,24},{24,28},{28,0},{1,5},{5... | collective-permute-start | bytes 1671176 | tf_op jit(solution)/shard_map/while/body/eval_jaxpr/ppermute | solution.py:17
  112.9 14.4 %collective-permute-start = (f32[128,1088]{0,1:T(8,128)}, f32[128,1088]{0,1:T(8,128)S(1)}, u32[]{:S(2)}, u32[]{:S(2)}) collective-permute-start(f32[128,1088]{0,1:T(8,128)} %maximum_add_fusion.3), channel_id=1, source_target_pairs={{0,4},{4,8},{8,12},{12,16},{16,20},{20,24},{24,28},{28,0},{1,5},{5... | collective-permute-start | bytes 1671176 | tf_op jit(solution)/shard_map/while/body/eval_jaxpr/ppermute | solution.py:17
  132.7 13.5 %collective-permute-start = (f32[128,1088]{0,1:T(8,128)}, f32[128,1088]{0,1:T(8,128)S(1)}, u32[]{:S(2)}, u32[]{:S(2)}) collective-permute-start(f32[128,1088]{0,1:T(8,128)} %maximum_add_fusion.3), channel_id=1, source_target_pairs={{0,4},{4,8},{8,12},{12,16},{16,20},{20,24},{24,28},{28,0},{1,5},{5... | collective-permute-start | bytes 1671176 | tf_op jit(solution)/shard_map/while/body/eval_jaxpr/ppermute | solution.py:17
  151.7 12.7 %collective-permute-start = (f32[128,1088]{0,1:T(8,128)}, f32[128,1088]{0,1:T(8,128)S(1)}, u32[]{:S(2)}, u32[]{:S(2)}) collective-permute-start(f32[128,1088]{0,1:T(8,128)} %maximum_add_fusion.3), channel_id=1, source_target_pairs={{0,4},{4,8},{8,12},{12,16},{16,20},{20,24},{24,28},{28,0},{1,5},{5... | collective-permute-start | bytes 1671176 | tf_op jit(solution)/shard_map/while/body/eval_jaxpr/ppermute | solution.py:17
  169.9 12.4 %collective-permute-start = (f32[128,1088]{0,1:T(8,128)}, f32[128,1088]{0,1:T(8,128)S(1)}, u32[]{:S(2)}, u32[]{:S(2)}) collective-permute-start(f32[128,1088]{0,1:T(8,128)} %maximum_add_fusion.3), channel_id=1, source_target_pairs={{0,4},{4,8},{8,12},{12,16},{16,20},{20,24},{24,28},{28,0},{1,5},{5... | collective-permute-start | bytes 1671176 | tf_op jit(solution)/shard_map/while/body/eval_jaxpr/ppermute | solution.py:17
  187.8 14.0 %collective-permute-start = (f32[128,1088]{0,1:T(8,128)}, f32[128,1088]{0,1:T(8,128)S(1)}, u32[]{:S(2)}, u32[]{:S(2)}) collective-permute-start(f32[128,1088]{0,1:T(8,128)} %maximum_add_fusion.3), channel_id=1, source_target_pairs={{0,4},{4,8},{8,12},{12,16},{16,20},{20,24},{24,28},{28,0},{1,5},{5... | collective-permute-start | bytes 1671176 | tf_op jit(solution)/shard_map/while/body/eval_jaxpr/ppermute | solution.py:17
  202.8 12.3 %collective-permute-start.1 = (f32[128,1088]{0,1:T(8,128)S(1)}, f32[128,1088]{0,1:T(8,128)S(1)}, u32[]{:S(2)}, u32[]{:S(2)}) collective-permute-start(f32[128,1088]{0,1:T(8,128)S(1)} %maximum_add_fusion.1), channel_id=1, source_target_pairs={{0,4},{4,8},{8,12},{12,16},{16,20},{20,24},{24,28},{28,0},{1,5},{5... | collective-permute-start | bytes 1671176 | tf_op jit(solution)/shard_map/ppermute | solution.py:17
  215.9 1.6 copy-start.3
  217.4 122.1 %all-reduce.3.cloned.1.call-start = ((), (), s32[]{:S(2)}) async-start(), calls=%async_computation.2 | async-start | bytes 4194304 | tf_op jit(solution)/shard_map/psum | solution.py:156
  339.5 2.6 copy-start.4
Sparse Core Ops, SparseCore 0:
  10.1 43.1 all-gather.4
  217.5 15.3 all-gather.6
  237.2 102.2 all-reduce.2
